TPU v7x, 32 devices: a whole 2x2x4 slice. The times are simulated.
32 devices in a mesh: patch: 8 (over z, x), rep: 4 (over y, core).
Axes of the slice: x: 2, y: 2, z: 4, core: 2. Of those that a mesh axis runs over, the one named last changes fastest.
Arguments:
- node_latents: bfloat16 [4, 3072, 512], P('rep', 'patch'), may hold values from -6 to 6
- edge_latents: bfloat16 [4, 10240, 512], P('rep', 'patch'), may hold values from -6 to 6
- targets: bfloat16 [4, 3072, 128], P('rep', 'patch'), may hold values from -6 to 6
- edge_weight_in: bfloat16 [1536, 512], replicated, may hold values from -0.15625 to 0.15625
- edge_weight_out: bfloat16 [512, 512], replicated, may hold values from -0.25 to 0.25
- node_weight_in: bfloat16 [1024, 512], replicated, may hold values from -0.1875 to 0.1875
- node_weight_out: bfloat16 [512, 512], replicated, may hold values from -0.25 to 0.25
- readout_weight: bfloat16 [512, 128], replicated, may hold values from -0.25 to 0.25
- send_rows: int32 [8, 96], P('patch'), may hold values from 0 to 383, as said below
- far_rows: int32 [8, 8], P('patch'), may hold values from 0 to 383, as said below
- edge_sender: int32 [10240], P('patch'), may hold values from 0 to 487
- edge_receiver: int32 [10240], P('patch'), may hold values from 0 to 383
- edge_count: int32 [8], P('patch'), may hold values from 80 to 1280, as said below
- land_mask: int32 [3072], P('patch'), may hold values 0 or 1
- lat_band: int32 [3072], P('patch'), may hold values from 0 to 720
Outputs:
- node_grad: bfloat16 [4, 3072, 512], P('rep', 'patch')
- edge_grad: bfloat16 [4, 10240, 512], P('rep', 'patch')
- grad_edge_in: float32 [1536, 512], P('patch')
- grad_edge_out: float32 [512, 512], P('patch')
- grad_node_in: float32 [1024, 512], P('patch')
- grad_node_out: float32 [512, 512], P('patch')
- grad_readout: float32 [512, 128], P('patch')
Inputs may be any that keep to these rules, and one draw needn't show every extreme that they name: `send_rows`: the 16 entries of a patch for one neighbour are distinct. `far_rows`: each patch sends exactly one node to every patch (itself included). `edge_count`: some patch has all 1280 edges live.
All inputs are finite; a program needn't handle non-finite values. No bound on the sum of `land_mask` on one device may be relied on, other than what follows from the above.
Results may differ from a plain program's by a relative error of at most 0.012.
Values may be sent and summed in bfloat16 or wider, within the bound.
A program may use at most 128 MiB of HBM per device.

v0:
```python
import functools

import jax
import jax.numpy as jnp
from jax import lax
from jax.experimental import pallas as pl
from jax.experimental.pallas import tpu as pltpu
from jax.sharding import PartitionSpec as P

OCEAN = 32
BANDS = 721
OFFSETS = (1, -1, 2, -2, 3, -3)
MESH = pl.DeviceIdType.MESH
F32 = jnp.float32
BF16 = jnp.bfloat16


def mm(left, right):
    return jnp.dot(left, right, preferred_element_type=F32)


def mm_left(left, right):
    return lax.dot_general(left, right, (((0,), (0,)), ((), ())), preferred_element_type=F32)


def mm_right(left, right):
    return lax.dot_general(left, right, (((1,), (1,)), ((), ())), preferred_element_type=F32)


def logistic(values):
    return 1.0 / (1.0 + jnp.exp(-values))


def mean(values):
    return jnp.mean(values, axis=-1, keepdims=True)


class Stream:
    def __init__(self, refs, order, sizes, patch, rep):
        self.order = order
        n = len(order)
        self.own, self.got, self.acc, self.fin = refs[0], refs[1 : 1 + n], refs[1 + n : 1 + 2 * n], refs[1 + 2 * n]
        self.send, self.recv = refs[2 + 2 * n :]
        self.sizes = sizes
        self.patch, self.rep = patch, rep
        self.at = {"side": lax.rem(rep, 2), "wide": lax.div(rep, 2), "low": lax.rem(patch, 2), "high": lax.div(patch, 2)}
        self.reps = sizes["side"] * sizes["wide"]
        self.sent, self.wait, self.slot, self.done = [], [], 0, 0

    def device(self, axis, index):
        at = dict(self.at)
        at[axis] = index
        return (2 * at["high"] + at["low"], 2 * at["wide"] + at["side"])

    def copy(self, src, dst, device):
        c = pltpu.make_async_remote_copy(
            src_ref=src, dst_ref=dst, send_sem=self.send.at[self.slot], recv_sem=self.recv.at[self.slot],
            device_id=device, device_id_type=MESH)
        c.start()
        self.slot += 1
        self.sent.append(c)
        self.wait.append(c)

    def arrive(self):
        for c in self.wait:
            c.wait_recv()
        self.wait = []

    def step(self):
        now, stages = self.done, len(self.order)
        held = self.own
        if now:
            self.arrive()
            axis = self.order[now - 1]
            before = self.own if now == 1 else self.acc[now - 2]
            total = before[self.at[axis]].astype(F32)
            for d in range(1, self.sizes[axis]):
                total = total + self.got[now - 1][d - 1].astype(F32)
            held = self.acc[now - 1]
            held[...] = total.astype(BF16)
        self.done += 1
        if now < stages:
            axis = self.order[now]
            for d in range(1, self.sizes[axis]):
                other = lax.rem(self.at[axis] + d, self.sizes[axis])
                self.copy(held.at[other], self.got[now].at[d - 1], self.device(axis, other))
            return
        mine = self.group(self.rep)
        self.fin[mine] = held[...]
        for other in self.lacking():
            self.copy(held, self.fin.at[mine], (self.patch, other))

    def group(self, rep):
        return rep if "wide" in self.order and "side" in self.order else 0

    def lacking(self):
        return [lax.rem(self.rep + d, self.reps) for d in range(1, self.reps)]

    def finish(self):
        self.arrive()
        for c in self.sent:
            c.wait_send()


class Small(Stream):
    def step(self):
        if self.done < len(self.order):
            return super().step()
        self.arrive()
        axis = self.order[-1]
        total = self.acc[-2][self.at[axis]].astype(F32)
        for d in range(1, self.sizes[axis]):
            total = total + self.got[-1][d - 1].astype(F32)
        self.acc[-1][...] = total.astype(BF16)
        self.fin[self.rep] = self.acc[-1][...]
        for other in self.lacking():
            self.copy(self.acc[-1], self.fin.at[self.rep], (self.patch, other))
        self.done += 1


ORDERS = (
    ("side", "low", "wide", "high"),
    ("side", "wide", "low", "high"),
    ("low", "high"),
    ("side", "low", "wide", "high"),
    ("side", "wide", "low", "high"),
)


def stream_scratch(rows, width, order, sizes):
    lead = tuple(sizes[a] for a in order)
    scratch = [pltpu.VMEM(lead + (rows, width), BF16)]
    slots = sizes["side"] * sizes["wide"] - 1
    for i, axis in enumerate(order):
        scratch.append(pltpu.VMEM((max(sizes[axis] - 1, 1),) + lead[i + 1 :] + (rows, width), BF16))
        slots += sizes[axis] - 1
    for i in range(len(order)):
        scratch.append(pltpu.VMEM(lead[i + 1 :] + (rows, width), BF16))
    scratch.append(pltpu.VMEM((sizes["side"] * sizes["wide"], rows, width), BF16))
    return scratch + [pltpu.SemaphoreType.DMA((slots,)), pltpu.SemaphoreType.DMA((slots,))]


def put(stream, row, value, low=0, rows=None):
    sizes, order = stream.sizes, stream.order
    patches = sizes["low"] * sizes["high"]
    block = value.shape[0] // patches
    rows = block - low if rows is None else rows
    pieces = stream.reps if "side" in order else 1
    width = value.shape[1] // pieces
    for p in range(patches):
        for r in range(pieces):
            at = {"side": r % 2, "wide": r // 2, "low": p % 2, "high": p // 2}
            stream.own[tuple(at[a] for a in order) + (slice(row, row + rows), slice(None))] = value[
                p * block + low : p * block + low + rows, r * width : (r + 1) * width
            ].astype(BF16)


def take(stream, row, rows, out, at, scale):
    if "side" not in stream.order:
        total = stream.fin[0].astype(F32)
        for r in range(1, stream.reps):
            total = total + stream.fin[r].astype(F32)
        out[...] = total * scale
        return
    width = out.shape[1] // stream.reps
    for r in range(stream.reps):
        out[at : at + rows, r * width : (r + 1) * width] = stream.fin[r, row : row + rows, :].astype(F32) * scale


def kernel(
    dims,
    x, e, tgt, w_ein, w_eout, w_nin, w_nout, w_ro, send_ids, far_ids, es, er, count, land, lat,
    o_node, o_edge, o_ein, o_eout, o_nin, o_nout, o_ro,
    near_out, near_in, far_out, far_in, back_near_out, back_near_in, back_far_out, back_far_in,
    xext, xw, table, sgrad, hid, msg, inv, ezg, epg, agg_grad, total,
    near_send, near_recv, far_send, far_recv, bn_send, bn_recv, bf_send, bf_recv,
    *stream_refs,
):
    patches, reps, slot, far, ext, tile = dims
    nodes, width = x.shape
    edges = e.shape[0]
    near = 6 * slot
    patch, rep = lax.axis_index("patch"), lax.axis_index("rep")
    sizes = {"side": 2, "wide": reps // 2, "low": 2, "high": patches // 2}
    streams, used = [], 0
    for order in ORDERS:
        count_refs = 4 + 2 * len(order)
        kind = Stream if "side" in order else Small
        streams.append(kind(stream_refs[used : used + count_refs], order, sizes, patch, rep))
        used += count_refs
    s_in, s_out, s_ro, s_one, s_two = streams

    barrier = pltpu.get_barrier_semaphore()
    for d in range(1, patches):
        pl.semaphore_signal(barrier, inc=1, device_id=(lax.rem(patch + d, patches), rep), device_id_type=MESH)
    for d in range(1, reps):
        pl.semaphore_signal(barrier, inc=1, device_id=(patch, lax.rem(rep + d, reps)), device_id_type=MESH)

    def listed(ids):
        hit = lax.broadcasted_iota(jnp.int32, (nodes, ids.shape[1]), 0) == ids[...]
        return jnp.where(hit, 1.0, 0.0).astype(BF16)

    own_near, own_far = listed(send_ids), listed(far_ids)
    outgoing, outgoing_far = mm_left(own_near, x[...]), mm_left(own_far, x[...])
    for k in range(6):
        near_out[k] = outgoing[k * slot : (k + 1) * slot].astype(BF16)
    for q in range(patches):
        far_out[q] = outgoing_far[q * far : (q + 1) * far].astype(BF16)
    pl.semaphore_wait(barrier, patches - 1 + reps - 1)

    def remote(src, dst, send, recv, device):
        c = pltpu.make_async_remote_copy(
            src_ref=src, dst_ref=dst, send_sem=send, recv_sem=recv, device_id=device, device_id_type=MESH)
        c.start()
        return c

    halo = []
    for k, o in enumerate(OFFSETS):
        to = lax.rem(patch + (o + patches), patches)
        halo.append(remote(near_out.at[k], near_in.at[k], near_send.at[k], near_recv.at[k], (to, rep)))
    for d in range(1, patches):
        to = lax.rem(patch + d, patches)
        halo.append(remote(far_out.at[to], far_in.at[patch], far_send.at[d - 1], far_recv.at[d - 1], (to, rep)))
    far_in[patch] = far_out[patch]

    w_s, w_r, w_e = (w_ein.at[pl.ds(i * width, width)] for i in range(3))
    xext[0:nodes, :] = x[...]
    xw[0:nodes, :] = mm(x[...], w_s[...]).astype(BF16)
    xw[ext : ext + nodes, :] = mm(x[...], w_r[...]).astype(BF16)

    def tables(t, _):
        at = pl.ds(pl.multiple_of(t * tile, tile), tile)
        hit = lax.broadcasted_iota(jnp.int32, (ext, tile), 0) == es[at][None, :]
        table[0:ext, at] = jnp.where(hit, 1.0, 0.0).astype(BF16)
        alive = lax.broadcasted_iota(jnp.int32, (1, tile), 1) + t * tile < count[0]
        ids = jnp.where(alive, er[at][None, :], -1)
        hit = lax.broadcasted_iota(jnp.int32, (nodes, tile), 0) == ids
        table[ext : ext + nodes, at] = jnp.where(hit, 1.0, 0.0).astype(BF16)
        sgrad[at, :] = mm(e[at, :], w_e[...])
        return 0

    lax.fori_loop(0, edges // tile, tables, 0)

    for c in halo:
        c.wait_recv()
    pieces = [near_in[k] for k in range(6)] + [far_in[q] for q in range(patches)]
    pad = ext - nodes - near - patches * far
    if pad:
        pieces.append(jnp.zeros((pad, width), BF16))
    arrived = jnp.concatenate([v.astype(F32) for v in pieces], axis=0).astype(BF16)
    xext[nodes:ext, :] = arrived
    xw[nodes:ext, :] = mm(arrived, w_s[...]).astype(BF16)

    def edge_forward(t, _):
        at = pl.ds(pl.multiple_of(t * tile, tile), tile)
        pre = sgrad[at, :] + mm_left(table[:, at], xw[...])
        s = logistic(pre)
        hidden = (pre * s).astype(BF16)
        sgrad[at, :] = s * (1.0 + pre * (1.0 - s))
        hid[at, :] = hidden
        z = mm(hidden, w_eout[...])
        centred = z - mean(z)
        inverse = lax.rsqrt(mean(centred * centred) + 1e-05)
        inv[at, :] = inverse
        msg[at, :] = (centred * inverse).astype(BF16)
        return 0

    lax.fori_loop(0, edges // tile, edge_forward, 0)

    variables = tgt.shape[1]
    latitude = -0.5 * jnp.pi + (lat[...].astype(F32) + 0.5) * (jnp.pi / BANDS)
    area = jnp.broadcast_to(jnp.cos(latitude)[None, :], (variables, nodes))
    ocean = lax.broadcasted_iota(jnp.int32, (variables, nodes), 0) < OCEAN
    masked = jnp.broadcast_to((land[...])[None, :], (variables, nodes)) == 1
    loss_weight = jnp.transpose(jnp.where(ocean & masked, 0.0, area))
    aggregate = mm(table[ext : ext + nodes, :], msg[...]).astype(BF16)
    node_pre = mm(x[...], w_nin[0:width, :]) + mm(aggregate, w_nin[width : 2 * width, :])
    s = logistic(node_pre)
    node_hidden = (node_pre * s).astype(BF16)
    node_sgrad = s * (1.0 + node_pre * (1.0 - s))
    z = mm(node_hidden, w_nout[...])
    centred = z - mean(z)
    inverse = lax.rsqrt(mean(centred * centred) + 1e-05)
    normed = centred * inverse
    updated = (x[...].astype(F32) + normed).astype(BF16)
    pred_grad = (loss_weight * (mm(updated, w_ro[...]) - tgt[...].astype(F32))).astype(BF16)
    up_grad = mm_right(pred_grad, w_ro[...])
    z_grad = (inverse * (up_grad - mean(up_grad) - normed * mean(up_grad * normed))).astype(BF16)
    pre_grad = (mm_right(z_grad, w_nout[...]) * node_sgrad).astype(BF16)
    total[...] = up_grad + mm_right(pre_grad, w_nin[0:width, :])
    agg_grad[...] = mm_right(pre_grad, w_nin[width : 2 * width, :]).astype(BF16)
    share = width // patches
    put(s_in, 0, jnp.concatenate([mm_left(x[...], pre_grad), mm_left(aggregate, pre_grad)], axis=0))
    s_in.step()
    put(s_out, 0, mm_left(node_hidden, z_grad))
    s_out.step()
    put(s_ro, 0, mm_left(updated, pred_grad))
    s_ro.step()

    def edge_backward(t, _):
        at = pl.ds(pl.multiple_of(t * tile, tile), tile)
        g = mm_left(table[ext : ext + nodes, at], agg_grad[...])
        y = msg[at, :].astype(F32)
        zg = (inv[at, :] * (g - mean(g) - y * mean(g * y))).astype(BF16)
        ezg[at, :] = zg
        epg[at, :] = (mm_right(zg, w_eout[...]) * sgrad[at, :]).astype(BF16)
        return 0

    steps = edges // tile
    cuts = [0, steps // 5, (2 * steps) // 5, (3 * steps) // 5, steps]
    lax.fori_loop(cuts[0], cuts[1], edge_backward, 0)
    s_in.step()
    s_out.step()
    lax.fori_loop(cuts[1], cuts[4], edge_backward, 0)
    s_out.step()
    s_in.step()
    s_ro.step()

    sums32 = mm(table[0:ext, :], epg[...])
    sums = sums32.astype(BF16)
    for k in range(6):
        back_near_out[k] = sums32[nodes + k * slot : nodes + (k + 1) * slot].astype(BF16)
    for q in range(patches):
        at = nodes + near + q * far
        back_far_out[q] = sums32[at : at + far].astype(BF16)
    back = []
    for k, o in enumerate(OFFSETS):
        to = lax.rem(patch + (patches - o), patches)
        back.append(remote(back_near_out.at[k], back_near_in.at[k], bn_send.at[k], bn_recv.at[k], (to, rep)))
    for d in range(1, patches):
        to = lax.rem(patch + d, patches)
        back.append(remote(back_far_out.at[to], back_far_in.at[patch], bf_send.at[d - 1], bf_recv.at[d - 1], (to, rep)))
    back_far_in[patch] = back_far_out[patch]
    rsums = mm(table[ext : ext + nodes, :], epg[...]).astype(BF16)
    put_in = jnp.concatenate(
        [mm_left(xext[...], sums), mm_left(x[...], rsums), mm_left(e[...], epg[...])], axis=0)
    put(s_two, 0, put_in, share)
    s_two.step()
    put(s_one, 0, put_in, 0, share)
    put(s_one, share, mm_left(hid[...], ezg[...]))
    s_one.step()
    s_two.step()
    s_one.step()
    s_out.step()
    s_in.step()
    total[...] += mm_right(rsums, w_r[...])

    def edge_out(t, _):
        at = pl.ds(pl.multiple_of(t * tile, tile), tile)
        o_edge[at, :] = mm_right(epg[at, :], w_e[...]).astype(BF16)
        return 0

    lax.fori_loop(0, steps, edge_out, 0)
    s_ro.step()
    s_in.step()
    s_out.step()
    for c in back:
        c.wait_recv()
    near_back = jnp.concatenate([back_near_in[k] for k in range(6)], axis=0)
    far_back = jnp.concatenate([back_far_in[q].astype(F32) for q in range(patches)], axis=0).astype(BF16)
    owned = mm(own_near, near_back) + mm(own_far, far_back)
    owned = (owned + sums32[0:nodes]).astype(BF16)
    o_node[...] = (total[...] + mm_right(owned, w_s[...])).astype(BF16)

    scale = 1.0 / (nodes * patches * reps)
    for _ in range(3):
        s_two.step()
        s_one.step()
    for c in halo + back:
        c.wait_send()
    s_in.finish()
    s_out.finish()
    s_ro.finish()
    take(s_in, 0, 2 * share, o_nin, 0, scale)
    take(s_out, 0, share, o_nout, 0, scale)
    take(s_ro, 0, share, o_ro, 0, scale)
    s_one.finish()
    take(s_one, 0, share, o_ein, 0, scale)
    take(s_one, share, share, o_eout, 0, scale)
    s_two.finish()
    take(s_two, 0, 2 * share, o_ein, share, scale)


def settle_kernel(n, *refs):
    src, dst, held = refs[:n], refs[n : 2 * n], refs[2 * n : 3 * n]
    sem_in, sem_out = refs[3 * n :]
    into = [pltpu.make_async_copy(src[i], held[i], sem_in.at[i]) for i in range(n)]
    out = [pltpu.make_async_copy(held[i], dst[i], sem_out.at[i]) for i in range(n)]
    for c in into:
        c.start()
    for i in range(n):
        into[i].wait()
        out[i].start()
    for c in out:
        c.wait()


def settle(arrays):
    n = len(arrays)
    hbm = pl.BlockSpec(memory_space=pl.ANY)
    return pl.pallas_call(
        functools.partial(settle_kernel, n),
        out_shape=tuple(jax.ShapeDtypeStruct(a.shape, a.dtype) for a in arrays),
        in_specs=[hbm] * n,
        out_specs=tuple([hbm] * n),
        scratch_shapes=[pltpu.VMEM(a.shape, a.dtype) for a in arrays]
        + [pltpu.SemaphoreType.DMA((n,)), pltpu.SemaphoreType.DMA((n,))],
    )(*arrays)


def call(
    node_latents, edge_latents, targets, edge_weight_in, edge_weight_out, node_weight_in, node_weight_out,
    readout_weight, send_rows, far_rows, edge_sender, edge_receiver, edge_count, land_mask, lat_band,
):
    nodes, width = node_latents.shape[1:]
    edges = edge_latents.shape[1]
    variables = targets.shape[2]
    patches, reps = lax.axis_size("patch"), lax.axis_size("rep")
    slot = send_rows.shape[1] // 6
    far = far_rows.shape[1] // patches
    near = 6 * slot
    remote_rows = near + patches * far
    ext = -(-(nodes + remote_rows) // 16) * 16
    tile = 256 if edges % 256 == 0 else 128
    share = width // patches
    vmem = pl.BlockSpec(memory_space=pltpu.VMEM)
    smem = pl.BlockSpec(memory_space=pltpu.SMEM)
    dma = lambda n: pltpu.SemaphoreType.DMA((n,))
    scratch = [
        pltpu.VMEM((6, slot, width), BF16), pltpu.VMEM((6, slot, width), BF16),
        pltpu.VMEM((patches, far, width), BF16), pltpu.VMEM((patches, far, width), BF16),
        pltpu.VMEM((6, slot, width), BF16), pltpu.VMEM((6, slot, width), BF16),
        pltpu.VMEM((patches, far, width), BF16), pltpu.VMEM((patches, far, width), BF16),
        pltpu.VMEM((ext, width), BF16),
        pltpu.VMEM((ext + nodes, width), BF16),
        pltpu.VMEM((ext + nodes, edges), BF16),
        pltpu.VMEM((edges, width), F32),
        pltpu.VMEM((edges, width), BF16),
        pltpu.VMEM((edges, width), BF16),
        pltpu.VMEM((edges, 1), F32),
        pltpu.VMEM((edges, width), BF16),
        pltpu.VMEM((edges, width), BF16),
        pltpu.VMEM((nodes, width), BF16),
        pltpu.VMEM((nodes, width), F32),
        dma(6), dma(6), dma(patches - 1), dma(patches - 1),
        dma(6), dma(6), dma(patches - 1), dma(patches - 1),
    ]
    sizes = {"side": 2, "wide": reps // 2, "low": 2, "high": patches // 2}
    for order, count in zip(ORDERS, (2 * share, share, share, 2 * share, 2 * share)):
        scratch += stream_scratch(count, width // reps if "side" in order else variables, order, sizes)
    shape = jax.ShapeDtypeStruct
    outs = pl.pallas_call(
        functools.partial(kernel, (patches, reps, slot, far, ext, tile)),
        out_shape=(
            shape((nodes, width), BF16), shape((edges, width), BF16),
            shape((3 * share, width), F32), shape((share, width), F32),
            shape((2 * share, width), F32), shape((share, width), F32), shape((share, variables), F32),
        ),
        in_specs=[vmem] * 12 + [smem] + [vmem] * 2,
        out_specs=tuple([vmem] * 7),
        scratch_shapes=scratch,
        compiler_params=pltpu.CompilerParams(
            collective_id=0, has_side_effects=True, vmem_limit_bytes=62 * 1024 * 1024),
    )(
        node_latents[0], edge_latents[0], targets[0], edge_weight_in, edge_weight_out, node_weight_in,
        node_weight_out, readout_weight, send_rows, far_rows, edge_sender, edge_receiver, edge_count,
        land_mask, lat_band,
    )
    outs = settle(outs)
    return (outs[0][None], outs[1][None]) + tuple(outs[2:])


def solution(mesh):
    rows = P("rep", "patch", None)
    in_specs = (rows,) * 3 + (P(),) * 5 + (P("patch", None),) * 2 + (P("patch"),) * 5
    out_specs = (rows,) * 2 + (P("patch", None),) * 5
    return jax.shard_map(call, mesh=mesh, in_specs=in_specs, out_specs=out_specs, check_vma=False)
```

profile of v0, /device:TPU:0, one launch (start us, length us, event | category | flops | bytes accessed | tf_op | source)
XLA Modules:
  0.0 64.4 jit_solution(5897662829371646562)
XLA Ops:
  1.3 60.2 %shard_map.198 = (bf16[384,512]{1,0:T(8,128)(2,1)}, bf16[1280,512]{1,0:T(8,128)(2,1)}, f32[192,512]{1,0:T(8,128)}, f32[64,512]{1,0:T(8,128)}, f32[128,512]{1,0:T...) custom-call(bf16[384,512]{1,0:T(8,128)(2,1)} %bitcast.6, bf16[1280,512]{1,0:T(8,128)(2,1)} %bitcast.5, ...), custom_call_target="tpu_custom_call" | custom-call | tf_op jit(solution)/shard_map/pallas_call | solution.py:452
  61.5 2.9 %shard_map.199 = (bf16[384,512]{1,0:T(8,128)(2,1)}, bf16[1280,512]{1,0:T(8,128)(2,1)}, f32[192,512]{1,0:T(8,128)}, f32[64,512]{1,0:T(8,128)}, f32[128,512]{1,0:T...) custom-call(bf16[384,512]{1,0:T(8,128)(2,1)} %get-tuple-element.21.refs_0_, bf16[1280,512]{1,0:T(8,128)(2,1)} %get-tuple-element.22.refs_1_, ...), custom_call_target="tpu_custom_call" | custom-call | tf_op jit(solution)/shard_map/pallas_call | solution.py:401
where the time goes:
time: 64.6 us; the launch traced here: 64.4 us
  Pallas kernels  63.2 us (98%)
  between operations  1.29 us (2%)
    pallas_call x1, Pallas kernels, call(): pl.pallas_call(functools.partial(kernel, (patches, reps, slot, far, ext,...  60.2 us
    pallas_call x1, Pallas kernels, settle(): pl.pallas_call(functools.partial(settle_kernel, n), out_shape=tuple((jax....  2.92 us

commit v1 on v0

v1 whole, which is shorter than its diff:
```python
import functools

import jax
import jax.numpy as jnp
from jax import lax
from jax.experimental import pallas as pl
from jax.experimental.pallas import tpu as pltpu
from jax.sharding import PartitionSpec as P

OCEAN = 32
BANDS = 721
OFFSETS = (1, -1, 2, -2, 3, -3)
MESH = pl.DeviceIdType.MESH
F32 = jnp.float32
BF16 = jnp.bfloat16


def mm(left, right):
    return jnp.dot(left, right, preferred_element_type=F32)


def mm_left(left, right):
    return lax.dot_general(left, right, (((0,), (0,)), ((), ())), preferred_element_type=F32)


def mm_right(left, right):
    return lax.dot_general(left, right, (((1,), (1,)), ((), ())), preferred_element_type=F32)


def logistic(values):
    return 0.5 * jnp.tanh(0.5 * values) + 0.5


def mean(values):
    return jnp.mean(values, axis=-1, keepdims=True)


def parse(kind):
    order = ("side",) + tuple(AXES[letter] for letter in kind if letter in AXES)
    return order, "W" in kind, "+" in kind


AXES = {"l": "low", "w": "wide", "h": "high"}


class Stream:
    def __init__(self, refs, kind, sizes, patch, rep):
        self.sizes, self.patch, self.rep = sizes, patch, rep
        self.order, self.sums, self.direct = parse(kind)
        n = len(self.order)
        self.own, self.got, self.acc = refs[0], refs[1 : 1 + n], refs[1 + n : 1 + 2 * n]
        self.last, self.fin, self.send, self.recv = refs[1 + 2 * n :]
        self.at = {"side": lax.rem(rep, 2), "wide": lax.div(rep, 2), "low": lax.rem(patch, 2), "high": lax.div(patch, 2)}
        self.sent, self.wait, self.done = None, None, 0

    def device(self, axis, index):
        at = dict(self.at)
        at[axis] = index
        return (2 * at["high"] + at["low"], 2 * at["wide"] + at["side"])

    def others(self, axis):
        size = self.sizes[axis]
        return [(d, lax.rem(self.at[axis] + d, size)) for d in range(1, size)]

    def peers(self, axis):
        return [self.device(axis, other) for _, other in self.others(axis)]

    def launch(self, ids, pairs, whole):
        if self.sent is not None:
            self.sent()
        copies = []
        for device, (src, dst) in zip(ids, pairs):
            copies.append(pltpu.make_async_remote_copy(
                src_ref=src, dst_ref=dst, send_sem=self.send.at[0], recv_sem=self.recv.at[self.done - 1],
                device_id=device, device_id_type=MESH))
            copies[-1].start()
        if len(copies) == 1:
            self.sent, self.wait = copies[0].wait_send, copies[0].wait_recv
        else:
            self.sent = pltpu.make_async_copy(whole, whole, self.send.at[0]).wait
            self.wait = pltpu.make_async_copy(whole, whole, self.recv.at[self.done - 1]).wait

    def arrive(self):
        if self.wait is not None:
            self.wait()
        self.wait = None

    def total(self, first, rest, count):
        if count == 1:
            return first + rest[0]
        value = first.astype(F32)
        for d in range(count):
            value = value + rest[d].astype(F32)
        return value.astype(BF16)

    def step(self):
        now, stages = self.done, len(self.order)
        self.done += 1
        held = self.own
        self.arrive()
        if 0 < now <= stages:
            axis = self.order[now - 1]
            before = self.own if now == 1 else self.acc[now - 2]
            held = self.acc[now - 1]
            held[...] = self.total(before[self.at[axis]], self.got[now - 1], self.sizes[axis] - 1)
        if now < stages:
            axis = self.order[now]
            pairs = [(held.at[other], self.got[now].at[d - 1]) for d, other in self.others(axis)]
            self.launch(self.peers(axis), pairs, self.got[now])
            return
        side, wide = self.at["side"], self.at["wide"]
        if self.direct:
            self.fin[side, wide] = held[...]
            reps = self.sizes["side"] * self.sizes["wide"]
            ids = [(self.patch, lax.rem(self.rep + d, reps)) for d in range(1, reps)]
            self.launch(ids, [(held, self.fin.at[side, wide])] * (reps - 1), self.last)
            return
        if now == stages:
            if not self.sums:
                self.fin[side, wide] = held[...]
            pairs = [
                (held, self.last.at[d - 1] if self.sums else self.fin.at[side, wide])
                for d, _ in self.others("wide")]
            self.launch(self.peers("wide"), pairs, self.last)
        elif now == stages + 1:
            if self.sums:
                self.fin[side] = self.total(self.acc[-1][...], self.last, self.sizes["wide"] - 1)
            self.launch(self.peers("side"), [(self.fin.at[side], self.fin.at[side])], None)

    def finish(self):
        self.sent()


def stream_scratch(kind, rows, width, sizes):
    order, sums, direct = parse(kind)
    lead = tuple(sizes[a] for a in order)
    scratch = [pltpu.VMEM(lead + (rows, width), BF16)]
    for i, axis in enumerate(order):
        scratch.append(pltpu.VMEM((max(sizes[axis] - 1, 1),) + lead[i + 1 :] + (rows, width), BF16))
    for i in range(len(order)):
        scratch.append(pltpu.VMEM(lead[i + 1 :] + (rows, width), BF16))
    last = sizes["side"] * sizes["wide"] - 1 if direct else max(sizes["wide"] - 1, 1)
    scratch.append(pltpu.VMEM((last, rows, width), BF16))
    fin = (sizes["side"],) if sums and not direct else (sizes["side"], sizes["wide"])
    scratch.append(pltpu.VMEM(fin + (rows, width), BF16))
    return scratch + [pltpu.SemaphoreType.DMA((1,)), pltpu.SemaphoreType.DMA((len(order) + 2,))]


def layout(stream, block):
    rows, width = stream.own.shape[-2:]
    by_row = block["by_row"]
    wides = 1 if stream.sums else stream.sizes["wide"]
    for side in range(2):
        for wide in range(wides):
            low = block["low"] + wide * rows + (side * rows * wides if by_row else 0)
            col = block["col"] + (0 if by_row else side * width)
            yield side, wide, low, col, rows, width


def put(stream, value, block):
    patches = stream.sizes["low"] * stream.sizes["high"]
    height = value.shape[0] // patches
    for p in range(patches):
        for side, wide, low, col, rows, width in layout(stream, block):
            at = {"side": side, "wide": wide, "low": p % 2, "high": p // 2}
            stream.own[tuple(at[a] for a in stream.order) + (slice(None), slice(None))] = value[
                p * height + low : p * height + low + rows, col : col + width
            ].astype(BF16)


def take(stream, out, block, scale, shift=0):
    for side, wide, low, col, rows, width in layout(stream, block):
        if stream.sums and stream.direct:
            held = stream.fin[side, 0].astype(F32)
            for w in range(1, stream.sizes["wide"]):
                held = held + stream.fin[side, w].astype(F32)
        else:
            held = (stream.fin[side] if stream.sums else stream.fin[side, wide]).astype(F32)
        out[low : low + rows, shift + col : shift + col + width] = held * scale


def stream_specs(share, width, variables):
    sides = {
        "ro": (share, variables), "no": (share, width), "ni": (2 * share, width), "eo": (share, width),
        "c0": (3 * share, width // 2), "c1": (3 * share, width // 2)}
    specs = []
    for group, down, across, kinds in STREAMS:
        height, columns = sides[group][0] // down, sides[group][1] // across
        by_row = group == "ro"
        for i, kind in enumerate(kinds):
            rows, cols = (height // 2, columns) if by_row else (height, columns // 2)
            place = {"low": (i // across) * height, "col": (i % across) * columns, "by_row": by_row}
            specs.append((f"{group}_{i}", kind, rows if parse(kind)[1] else rows // 2, cols, place))
    return specs


def kernel(
    dims,
    x_h, e_h, tgt_h, wein_h, weout_h, wnin_h, wnout_h, wro_h, send_h, far_h, es_h, er_h, count_h, land_h, lat_h,
    o_node, o_edge, o_ein, o_eout, o_nin, o_nout, o_ro,
    x, e, tgt, w_ein, w_eout, w_nin, w_nout, w_ro, send_ids, far_ids, es, er, count, land, lat, loaded,
    near_out, near_in, far_out, far_in, back_near_out, back_near_in, back_far_out, back_far_in,
    xext, xw, table, sgrad, hid, msg, inv, ezg, epg, agg_grad, total, sums, rsums, local, loss_weight,
    halo_sems, back_sems,
    *stream_refs,
):
    patches, reps, slot, far, ext, tile = dims
    nodes, width = x.shape
    edges = e.shape[0]
    near = 6 * slot
    share = width // patches
    half = width // 2
    patch, rep = lax.axis_index("patch"), lax.axis_index("rep")
    sizes = {"side": 2, "wide": reps // 2, "low": 2, "high": patches // 2}

    barrier = pltpu.get_barrier_semaphore()
    for d in range(1, patches):
        pl.semaphore_signal(barrier, inc=1, device_id=(lax.rem(patch + d, patches), rep), device_id_type=MESH)
    for d in range(1, reps):
        pl.semaphore_signal(barrier, inc=1, device_id=(patch, lax.rem(rep + d, reps)), device_id_type=MESH)

    loads = {}
    order = ("x", "send", "far", "wein", "er", "es", "count", "e", "weout", "wnin", "wnout", "wro", "tgt", "land", "lat")
    source = dict(
        x=(x_h, x), send=(send_h, send_ids), far=(far_h, far_ids), wein=(wein_h, w_ein), er=(er_h, er), es=(es_h, es),
        count=(count_h, count), e=(e_h, e), weout=(weout_h, w_eout), wnin=(wnin_h, w_nin), wnout=(wnout_h, w_nout),
        wro=(wro_h, w_ro), tgt=(tgt_h, tgt), land=(land_h, land), lat=(lat_h, lat))
    for i, name in enumerate(order):
        loads[name] = pltpu.make_async_copy(source[name][0], source[name][1], loaded.at[i])
        loads[name].start()

    specs = stream_specs(share, width, tgt.shape[1])
    streams, used = [], 0
    for _, kind, _, _, _ in specs:
        refs = 5 + 2 * len(parse(kind)[0])
        streams.append(Stream(stream_refs[used : used + refs], kind, sizes, patch, rep))
        used += refs
    named = {spec[0]: s for s, spec in zip(streams, specs)}
    groups = {}
    for s, spec in zip(streams, specs):
        groups.setdefault(spec[0][:2], []).append((s, spec[4]))

    def put_group(group, value):
        for s, place in groups[group]:
            put(s, value, place)
            s.step()

    returned = []

    def send_back():
        for k in range(6):
            back_near_out[k] = sums[nodes + k * slot : nodes + (k + 1) * slot, :]
        for q in range(patches):
            low = nodes + near + q * far
            back_far_out[q] = sums[low : low + far, :]
        returned.extend(exchange(-1, back_near_out, back_near_in, back_far_out, back_far_in, back_sems))

    def node_out():
        for c in returned[1]:
            c.wait()
        near_back = jnp.concatenate([back_near_in[k] for k in range(6)], axis=0)
        far_back = jnp.concatenate([back_far_in[q].astype(F32) for q in range(patches)], axis=0).astype(BF16)
        owned = mm(own_near, near_back) + mm(own_far, far_back)
        owned = (owned + local[...]).astype(BF16)
        o_node[...] = (total[...] + mm_right(owned, w_s[...])).astype(BF16)

    actions = {"back": send_back, "node": node_out}
    plan = iter(PLAN)

    def tick():
        for name in next(plan):
            if name in actions:
                actions[name]()
                continue
            named[name].step()

    def listed(ids):
        hit = lax.broadcasted_iota(jnp.int32, (nodes, ids.shape[1]), 0) == ids[...]
        return jnp.where(hit, 1.0, 0.0).astype(BF16)

    for name in ("x", "send", "far"):
        loads[name].wait()
    own_near, own_far = listed(send_ids), listed(far_ids)
    outgoing, outgoing_far = mm_left(own_near, x[...]), mm_left(own_far, x[...])
    for k in range(6):
        near_out[k] = outgoing[k * slot : (k + 1) * slot].astype(BF16)
    for q in range(patches):
        far_out[q] = outgoing_far[q * far : (q + 1) * far].astype(BF16)
    pl.semaphore_wait(barrier, patches - 1 + reps - 1)

    def remote(src, dst, send, recv, device):
        c = pltpu.make_async_remote_copy(
            src_ref=src, dst_ref=dst, send_sem=send, recv_sem=recv, device_id=device, device_id_type=MESH)
        c.start()
        return c

    def exchange(sign, near_from, near_to, far_from, far_to, sems):
        near_send, near_recv, far_send, far_recv = (sems.at[i] for i in range(4))
        for d in range(1, patches):
            to = lax.rem(patch + d, patches)
            remote(far_from.at[to], far_to.at[patch], far_send, far_recv, (to, rep))
        for k, o in reversed(tuple(enumerate(OFFSETS))):
            remote(near_from.at[k], near_to.at[k], near_send, near_recv, (lax.rem(patch + (sign * o + patches), patches), rep))
        far_to[patch] = far_from[patch]
        others = far_from.at[pl.ds(0, patches - 1)]
        return (
            [pltpu.make_async_copy(near_from, near_from, near_send), pltpu.make_async_copy(others, others, far_send)],
            [pltpu.make_async_copy(near_to, near_to, near_recv), pltpu.make_async_copy(others, others, far_recv)])

    halo_sent, halo = exchange(1, near_out, near_in, far_out, far_in, halo_sems)

    w_s, w_r, w_e = (w_ein.at[pl.ds(i * width, width)] for i in range(3))
    loads["wein"].wait()
    xext[0:nodes, :] = x[...]
    xw[0:nodes, :] = mm(x[...], w_s[...]).astype(BF16)
    xw[nodes : 2 * nodes, :] = mm(x[...], w_r[...]).astype(BF16)
    own, far_rows = 2 * nodes, ext - nodes

    for name in ("er", "es", "count", "e"):
        loads[name].wait()

    def tables(t):
        at = slice(t * tile, (t + 1) * tile)
        ids = es[at][None, :]
        hit = lax.broadcasted_iota(jnp.int32, (nodes, tile), 0) == ids
        table[0:nodes, at] = jnp.where(hit, 1.0, 0.0).astype(BF16)
        hit = lax.broadcasted_iota(jnp.int32, (far_rows, tile), 0) + nodes == ids
        table[own : own + far_rows, at] = jnp.where(hit, 1.0, 0.0).astype(BF16)
        alive = lax.broadcasted_iota(jnp.int32, (1, tile), 1) + t * tile < count[0]
        ids = jnp.where(alive, er[at][None, :], -1)
        hit = lax.broadcasted_iota(jnp.int32, (nodes, tile), 0) == ids
        table[nodes : 2 * nodes, at] = jnp.where(hit, 1.0, 0.0).astype(BF16)

    def edge_local(t):
        at = slice(t * tile, (t + 1) * tile)
        sgrad[at, :] = mm(e[at, :], w_e[...]) + mm_left(table[0:own, at], xw[0:own, :])

    parts = range(edges // tile)
    for t in parts:
        tables(t)
        edge_local(t)

    for name in order[8:]:
        loads[name].wait()
    variables = tgt.shape[1]
    latitude = -0.5 * jnp.pi + (lat[...].astype(F32) + 0.5) * (jnp.pi / BANDS)
    area = jnp.broadcast_to(jnp.cos(latitude)[None, :], (variables, nodes))
    ocean = lax.broadcasted_iota(jnp.int32, (variables, nodes), 0) < OCEAN
    masked = jnp.broadcast_to((land[...])[None, :], (variables, nodes)) == 1
    loss_weight[...] = jnp.transpose(jnp.where(ocean & masked, 0.0, area))
    total[...] = mm(x[...], w_nin[0:width, :])

    for c in halo:
        c.wait()
    pieces = [near_in[k] for k in range(6)] + [far_in[q] for q in range(patches)]
    pad = ext - nodes - near - patches * far
    if pad:
        pieces.append(jnp.zeros((pad, width), BF16))
    arrived = jnp.concatenate([v.astype(F32) for v in pieces], axis=0).astype(BF16)
    xext[nodes:ext, :] = arrived
    xw[own : own + far_rows, :] = mm(arrived, w_s[...]).astype(BF16)

    def edge_hidden(t):
        at = slice(t * tile, (t + 1) * tile)
        pre = sgrad[at, :] + mm_left(table[own : own + far_rows, at], xw[own : own + far_rows, :])
        s = logistic(pre)
        h = pre * s
        sgrad[at, :] = s + h * (1.0 - s)
        hid[at, :] = h.astype(BF16)

    def edge_normed(t):
        at = slice(t * tile, (t + 1) * tile)
        z = mm(hid[at, :], w_eout[...])
        centred = z - mean(z)
        inverse = lax.rsqrt(mean(centred * centred) + 1e-05)
        inv[at, :] = inverse
        msg[at, :] = (centred * inverse).astype(BF16)

    for t in parts:
        edge_hidden(t)
        edge_normed(t)

    aggregate = mm(table[nodes : 2 * nodes, :], msg[...]).astype(BF16)
    node_pre = total[...] + mm(aggregate, w_nin[width : 2 * width, :])
    s = logistic(node_pre)
    h = node_pre * s
    node_hidden = h.astype(BF16)
    node_sgrad = s + h * (1.0 - s)
    z = mm(node_hidden, w_nout[...])
    centred = z - mean(z)
    inverse = lax.rsqrt(mean(centred * centred) + 1e-05)
    normed = centred * inverse
    updated = (x[...].astype(F32) + normed).astype(BF16)
    pred_grad = (loss_weight[...] * (mm(updated, w_ro[...]) - tgt[...].astype(F32))).astype(BF16)
    up_grad = mm_right(pred_grad, w_ro[...])
    z_grad = (inverse * (up_grad - mean(up_grad) - normed * mean(up_grad * normed))).astype(BF16)
    put_group("no", mm_left(node_hidden, z_grad))
    tick()
    pre_grad = (mm_right(z_grad, w_nout[...]) * node_sgrad).astype(BF16)
    put_group("ni", jnp.concatenate([mm_left(x[...], pre_grad), mm_left(aggregate, pre_grad)], axis=0))
    tick()
    total[...] = up_grad + mm_right(pre_grad, w_nin[0:width, :])
    message_grad = mm_right(pre_grad, w_nin[width : 2 * width, :])
    agg_grad[...] = (message_grad - mean(message_grad)).astype(BF16)
    put_group("ro", mm_left(updated, pred_grad))
    tick()

    def edge_backward(t):
        at = slice(t * edges // 2, (t + 1) * edges // 2)
        g = mm_left(table[nodes : 2 * nodes, at], agg_grad[...])
        y = msg[at, :].astype(F32)
        zg = (inv[at, :] * (g - y * mean(g * y))).astype(BF16)
        ezg[at, :] = zg
        epg[at, :] = (mm_right(zg, w_eout[...]) * sgrad[at, :]).astype(BF16)

    for t in range(2):
        edge_backward(t)
        tick()
    put_group("eo", mm_left(hid[...], ezg[...]))
    tick()

    for c, group in enumerate(("c0", "c1")):
        at = pl.ds(c * half, half)
        sums32 = mm(table[0:nodes, :], epg[:, at])
        local[:, at] = sums32
        sums[0:nodes, at] = sums32.astype(BF16)
        sums[nodes:ext, at] = mm(table[own : own + far_rows, :], epg[:, at]).astype(BF16)
        tick()
        rsums[:, at] = mm(table[nodes : 2 * nodes, :], epg[:, at]).astype(BF16)
        tick()
        first = mm_left(e[...], epg[:, at])
        tick()
        put_group(group, jnp.concatenate(
            [mm_left(xext[...], sums[:, at]), mm_left(x[...], rsums[:, at]), first], axis=0))
        tick()

    for t in range(2):
        at = slice(t * edges // 2, (t + 1) * edges // 2)
        o_edge[at, :] = mm_right(epg[at, :], w_e[...]).astype(BF16)
        tick()
    total[...] += mm_right(rsums[...], w_r[...])
    tick()
    for s in streams:
        assert s.done == len(s.order) + (1 if s.direct else 2)

    scale = 1.0 / (nodes * patches * reps)
    for c in halo_sent + returned[0]:
        c.wait()
    into = {"ro": (o_ro, 0), "no": (o_nout, 0), "ni": (o_nin, 0), "eo": (o_eout, 0), "c0": (o_ein, 0), "c1": (o_ein, half)}
    for group, members in groups.items():
        for s, place in members:
            s.arrive()
            take(s, into[group][0], place, scale, into[group][1])
    for s in streams:
        s.finish()


STREAMS = (
    ("ro", 1, 1, ("wlh",)),
    ("no", 1, 2, ("hlw+", "wlh")),
    ("ni", 1, 2, ("hwl", "lwh+")),
    ("eo", 1, 2, ("wlh+", "lhW")),
    ("c0", 3, 1, ("wlh+", "lhW+", "wlh+")),
    ("c1", 3, 1, ("lwh+", "wlh", "wlh+")),
)


PLAN = (
    (),
    ("no_0",),
    ("no_1",),
    ("ni_0", "ni_1", "ro_0"),
    (),
    ("no_1",),
    ("ro_0",),
    (),
    ("eo_0", "no_0"),
    ("eo_1", "ni_1"),
    (),
    ("no_1", "ro_0", "back"),
    ("c0_0", "no_0", "c0_1", "c0_2"),
    ("eo_0",),
    ("eo_1", "ni_1"),
    ("c1_0", "c1_1", "c1_2", "ni_0"),
    ("c0_0", "no_0", "no_1", "ro_0", "c0_1", "c0_2", "eo_0", "c1_1", "node", "c1_0", "c0_0", "eo_1", "c1_2",
     "c0_2", "ni_0", "ni_1", "c1_1", "no_1", "ro_0", "c1_0", "eo_1", "c0_1", "c1_2", "ni_0", "eo_0", "c0_0",
     "c0_2", "c1_1", "ni_0", "c1_0", "c1_2", "c1_1"),
)


def settle_kernel(n, *refs):
    src, dst, sem = refs[:n], refs[n : 2 * n], refs[2 * n]
    copies = [pltpu.make_async_copy(src[i], dst[i], sem.at[i]) for i in range(n)]
    for c in copies:
        c.start()
    for c in copies:
        c.wait()


def settle(arrays):
    n = len(arrays)
    return pl.pallas_call(
        functools.partial(settle_kernel, n),
        out_shape=tuple(jax.ShapeDtypeStruct(a.shape, a.dtype) for a in arrays),
        in_specs=[pl.BlockSpec(memory_space=pltpu.VMEM)] * n,
        out_specs=tuple([pl.BlockSpec(memory_space=pltpu.HBM)] * n),
        scratch_shapes=[pltpu.SemaphoreType.DMA((n,))],
        compiler_params=pltpu.CompilerParams(vmem_limit_bytes=4 * 1024 * 1024),
    )(*arrays)


def call(
    node_latents, edge_latents, targets, edge_weight_in, edge_weight_out, node_weight_in, node_weight_out,
    readout_weight, send_rows, far_rows, edge_sender, edge_receiver, edge_count, land_mask, lat_band,
):
    nodes, width = node_latents.shape[1:]
    edges = edge_latents.shape[1]
    variables = targets.shape[2]
    patches, reps = lax.axis_size("patch"), lax.axis_size("rep")
    slot = send_rows.shape[1] // 6
    far = far_rows.shape[1] // patches
    near = 6 * slot
    remote_rows = near + patches * far
    ext = -(-(nodes + remote_rows) // 16) * 16
    tile = edges
    share = width // patches
    vmem = pl.BlockSpec(memory_space=pltpu.VMEM)
    hbm = pl.BlockSpec(memory_space=pltpu.HBM)
    dma = lambda n: pltpu.SemaphoreType.DMA((n,))
    args = (
        node_latents[0], edge_latents[0], targets[0], edge_weight_in, edge_weight_out, node_weight_in,
        node_weight_out, readout_weight, send_rows, far_rows, edge_sender, edge_receiver, edge_count,
        land_mask, lat_band)
    scratch = [(pltpu.SMEM if i == 12 else pltpu.VMEM)(a.shape, a.dtype) for i, a in enumerate(args)] + [dma(len(args))]
    scratch += [
        pltpu.VMEM((6, slot, width), BF16), pltpu.VMEM((6, slot, width), BF16),
        pltpu.VMEM((patches, far, width), BF16), pltpu.VMEM((patches, far, width), BF16),
        pltpu.VMEM((6, slot, width), BF16), pltpu.VMEM((6, slot, width), BF16),
        pltpu.VMEM((patches, far, width), BF16), pltpu.VMEM((patches, far, width), BF16),
        pltpu.VMEM((ext, width), BF16),
        pltpu.VMEM((ext + nodes, width), BF16),
        pltpu.VMEM((ext + nodes, edges), BF16),
        pltpu.VMEM((edges, width), F32),
        pltpu.VMEM((edges, width), BF16),
        pltpu.VMEM((edges, width), BF16),
        pltpu.VMEM((edges, 1), F32),
        pltpu.VMEM((edges, width), BF16),
        pltpu.VMEM((edges, width), BF16),
        pltpu.VMEM((nodes, width), BF16),
        pltpu.VMEM((nodes, width), F32),
        pltpu.VMEM((ext, width), BF16),
        pltpu.VMEM((nodes, width), BF16),
        pltpu.VMEM((nodes, width), F32),
        pltpu.VMEM((nodes, variables), F32),
        dma(4), dma(4),
    ]
    sizes = {"side": 2, "wide": reps // 2, "low": 2, "high": patches // 2}
    for _, kind, rows, columns, _ in stream_specs(share, width, variables):
        scratch += stream_scratch(kind, rows, columns, sizes)
    shape = pltpu.VMEM
    args = tuple(a if i == 12 else pltpu.with_memory_space_constraint(a, pltpu.HBM) for i, a in enumerate(args))
    outs = pl.pallas_call(
        functools.partial(kernel, (patches, reps, slot, far, ext, tile)),
        out_shape=(
            shape((nodes, width), BF16), shape((edges, width), BF16),
            shape((3 * share, width), F32), shape((share, width), F32),
            shape((2 * share, width), F32), shape((share, width), F32), shape((share, variables), F32),
        ),
        in_specs=[hbm] * len(args),
        out_specs=tuple([vmem] * 7),
        scratch_shapes=scratch,
        compiler_params=pltpu.CompilerParams(
            collective_id=0, has_side_effects=True, vmem_limit_bytes=40 * 1024 * 1024),
    )(*args)
    outs = settle(outs)
    return (outs[0][None], outs[1][None]) + tuple(outs[2:])


def solution(mesh):
    rows = P("rep", "patch", None)
    in_specs = (rows,) * 3 + (P(),) * 5 + (P("patch", None),) * 2 + (P("patch"),) * 5
    out_specs = (rows,) * 2 + (P("patch", None),) * 5
    return jax.shard_map(call, mesh=mesh, in_specs=in_specs, out_specs=out_specs, check_vma=False)
```

time: 64.6 us -> 47.2 us (0.73)
  Pallas kernels: 63.2 us -> 45.6 us
    pallas_call x1, Pallas kernels: 60.2 us -> 44 us  [call(): pl.pallas_call(functools.partial(kernel, (patches, reps, slot, far, ext,...]
    pallas_call x1, Pallas kernels: 2.92 us -> 1.54 us  [settle(): pl.pallas_call(functools.partial(settle_kernel, n), out_shape=tuple((jax....]
where the time goes in v1:
time: 47.2 us; the launch traced here: 47 us
  Pallas kernels  45.6 us (97%)
  between operations  1.45 us (3%)
    pallas_call x1, Pallas kernels, call(): pl.pallas_call(functools.partial(kernel, (patches, reps, slot, far, ext,...  44 us
    pallas_call x1, Pallas kernels, settle(): pl.pallas_call(functools.partial(settle_kernel, n), out_shape=tuple((jax....  1.54 us

profile of v1, /device:TPU:0, one launch (start us, length us, event | category | flops | bytes accessed | tf_op | source)
XLA Modules:
  0.0 47.0 jit_solution(4477024249098677349)
XLA Ops:
  1.3 44.0 %shard_map.198 = (bf16[384,512]{1,0:T(8,128)(2,1)S(1)}, bf16[1280,512]{1,0:T(8,128)(2,1)S(1)}, f32[192,512]{1,0:T(8,128)S(1)}, f32[64,512]{1,0:T(8,128)S(1)}, f3...) custom-call(bf16[384,512]{1,0:T(8,128)(2,1)} %bitcast.6, bf16[1280,512]{1,0:T(8,128)(2,1)} %bitcast.5, ...), custom_call_target="tpu_custom_call" | custom-call | tf_op jit(solution)/shard_map/pallas_call | solution.py:562
  45.3 1.5 %shard_map.199 = (bf16[384,512]{1,0:T(8,128)(2,1)}, bf16[1280,512]{1,0:T(8,128)(2,1)}, f32[192,512]{1,0:T(8,128)}, f32[64,512]{1,0:T(8,128)}, f32[128,512]{1,0:T...) custom-call(bf16[384,512]{1,0:T(8,128)(2,1)S(1)} %get-tuple-element.21.refs_0_, ...), custom_call_target="tpu_custom_call" | custom-call | tf_op jit(solution)/shard_map/pallas_call | solution.py:502

commit v2 on v1

--- a/solution.py
+++ b/solution.py
@@ -9,7 +9,6 @@
 
 OCEAN = 32
 BANDS = 721
-OFFSETS = (1, -1, 2, -2, 3, -3)
 MESH = pl.DeviceIdType.MESH
 F32 = jnp.float32
 BF16 = jnp.bfloat16
@@ -98,6 +97,9 @@
         self.done += 1
         held = self.own
         self.arrive()
+        self.complete = now == stages + (1 if self.direct else 2)
+        if self.complete:
+            return
         if 0 < now <= stages:
             axis = self.order[now - 1]
             before = self.own if now == 1 else self.acc[now - 2]
@@ -143,7 +145,7 @@
     scratch.append(pltpu.VMEM((last, rows, width), BF16))
     fin = (sizes["side"],) if sums and not direct else (sizes["side"], sizes["wide"])
     scratch.append(pltpu.VMEM(fin + (rows, width), BF16))
-    return scratch + [pltpu.SemaphoreType.DMA((1,)), pltpu.SemaphoreType.DMA((len(order) + 2,))]
+    return scratch + [pltpu.SemaphoreType.DMA((1,)), pltpu.SemaphoreType.DMA((len(order) + (1 if direct else 2),))]
 
 
 def layout(stream, block):
@@ -201,6 +203,7 @@
     x, e, tgt, w_ein, w_eout, w_nin, w_nout, w_ro, send_ids, far_ids, es, er, count, land, lat, loaded,
     near_out, near_in, far_out, far_in, back_near_out, back_near_in, back_far_out, back_far_in,
     xext, xw, table, sgrad, hid, msg, inv, ezg, epg, agg_grad, total, sums, rsums, local, loss_weight,
+    aggregate, node_hidden, z_grad, updated, pred_grad, up_grad, node_sgrad,
     halo_sems, back_sems,
     *stream_refs,
 ):
@@ -264,6 +267,9 @@
         owned = (owned + local[...]).astype(BF16)
         o_node[...] = (total[...] + mm_right(owned, w_s[...])).astype(BF16)
 
+    scale = 1.0 / (nodes * patches * reps)
+    into = {"ro": (o_ro, 0), "no": (o_nout, 0), "ni": (o_nin, 0), "eo": (o_eout, 0), "c0": (o_ein, 0), "c1": (o_ein, half)}
+    places = {spec[0]: spec[4] for spec in specs}
     actions = {"back": send_back, "node": node_out}
     plan = iter(PLAN)
 
@@ -273,6 +279,9 @@
                 actions[name]()
                 continue
             named[name].step()
+            if named[name].complete:
+                out, shift = into[name[:2]]
+                take(named[name], out, places[name], scale, shift)
 
     def listed(ids):
         hit = lax.broadcasted_iota(jnp.int32, (nodes, ids.shape[1]), 0) == ids[...]
@@ -299,8 +308,14 @@
         for d in range(1, patches):
             to = lax.rem(patch + d, patches)
             remote(far_from.at[to], far_to.at[patch], far_send, far_recv, (to, rep))
-        for k, o in reversed(tuple(enumerate(OFFSETS))):
-            remote(near_from.at[k], near_to.at[k], near_send, near_recv, (lax.rem(patch + (sign * o + patches), patches), rep))
+        upper = lax.div(patch, patches // 2)
+        if sign < 0:
+            upper = 1 - upper
+        for m, down in ((1, 1), (2, 1), (3, 1), (3, 0), (2, 0), (1, 0)):
+            down = 1 - upper if down else upper
+            k = 2 * (m - 1) + down
+            to = lax.rem(patch + sign * m * (1 - 2 * down) + patches, patches)
+            remote(near_from.at[k], near_to.at[k], near_send, near_recv, (to, rep))
         far_to[patch] = far_from[patch]
         others = far_from.at[pl.ds(0, patches - 1)]
         return (
@@ -361,7 +376,7 @@
     xw[own : own + far_rows, :] = mm(arrived, w_s[...]).astype(BF16)
 
     def edge_hidden(t):
-        at = slice(t * tile, (t + 1) * tile)
+        at = slice(t * edges // 2, (t + 1) * edges // 2)
         pre = sgrad[at, :] + mm_left(table[own : own + far_rows, at], xw[own : own + far_rows, :])
         s = logistic(pre)
         h = pre * s
@@ -369,40 +384,54 @@
         hid[at, :] = h.astype(BF16)
 
     def edge_normed(t):
-        at = slice(t * tile, (t + 1) * tile)
+        at = slice(t * edges // 2, (t + 1) * edges // 2)
         z = mm(hid[at, :], w_eout[...])
         centred = z - mean(z)
         inverse = lax.rsqrt(mean(centred * centred) + 1e-05)
         inv[at, :] = inverse
         msg[at, :] = (centred * inverse).astype(BF16)
 
-    for t in parts:
+    for t in range(2):
         edge_hidden(t)
+    for t in range(2):
         edge_normed(t)
 
-    aggregate = mm(table[nodes : 2 * nodes, :], msg[...]).astype(BF16)
-    node_pre = total[...] + mm(aggregate, w_nin[width : 2 * width, :])
-    s = logistic(node_pre)
-    h = node_pre * s
-    node_hidden = h.astype(BF16)
-    node_sgrad = s + h * (1.0 - s)
-    z = mm(node_hidden, w_nout[...])
-    centred = z - mean(z)
-    inverse = lax.rsqrt(mean(centred * centred) + 1e-05)
-    normed = centred * inverse
-    updated = (x[...].astype(F32) + normed).astype(BF16)
-    pred_grad = (loss_weight[...] * (mm(updated, w_ro[...]) - tgt[...].astype(F32))).astype(BF16)
-    up_grad = mm_right(pred_grad, w_ro[...])
-    z_grad = (inverse * (up_grad - mean(up_grad) - normed * mean(up_grad * normed))).astype(BF16)
-    put_group("no", mm_left(node_hidden, z_grad))
+    aggregate[...] = mm(table[nodes : 2 * nodes, :], msg[...]).astype(BF16)
+
+    def node_part(low, high):
+        at = slice(low, high)
+        node_pre = total[at, :] + mm(aggregate[at, :], w_nin[width : 2 * width, :])
+        s = logistic(node_pre)
+        h = node_pre * s
+        node_hidden[at, :] = h.astype(BF16)
+        node_sgrad[at, :] = s + h * (1.0 - s)
+        yield
+        z = mm(node_hidden[at, :], w_nout[...])
+        centred = z - mean(z)
+        inverse = lax.rsqrt(mean(centred * centred) + 1e-05)
+        normed = centred * inverse
+        updated[at, :] = (x[at, :].astype(F32) + normed).astype(BF16)
+        yield
+        pred_grad[at, :] = (loss_weight[at, :] * (mm(updated[at, :], w_ro[...]) - tgt[at, :].astype(F32))).astype(BF16)
+        yield
+        up = mm_right(pred_grad[at, :], w_ro[...])
+        up_grad[at, :] = up
+        z_grad[at, :] = (inverse * (up - mean(up) - normed * mean(up * normed))).astype(BF16)
+        yield
+
+    node_parts = [node_part(0, nodes // 2), node_part(nodes // 2, nodes)]
+    for _ in range(4):
+        for part in node_parts:
+            next(part)
+    put_group("no", mm_left(node_hidden[...], z_grad[...]))
     tick()
-    pre_grad = (mm_right(z_grad, w_nout[...]) * node_sgrad).astype(BF16)
-    put_group("ni", jnp.concatenate([mm_left(x[...], pre_grad), mm_left(aggregate, pre_grad)], axis=0))
+    pre_grad = (mm_right(z_grad[...], w_nout[...]) * node_sgrad[...]).astype(BF16)
+    put_group("ni", jnp.concatenate([mm_left(x[...], pre_grad), mm_left(aggregate[...], pre_grad)], axis=0))
     tick()
-    total[...] = up_grad + mm_right(pre_grad, w_nin[0:width, :])
+    total[...] = up_grad[...] + mm_right(pre_grad, w_nin[0:width, :])
     message_grad = mm_right(pre_grad, w_nin[width : 2 * width, :])
     agg_grad[...] = (message_grad - mean(message_grad)).astype(BF16)
-    put_group("ro", mm_left(updated, pred_grad))
+    put_group("ro", mm_left(updated[...], pred_grad[...]))
     tick()
 
     def edge_backward(t):
@@ -440,51 +469,44 @@
         tick()
     total[...] += mm_right(rsums[...], w_r[...])
     tick()
-    for s in streams:
-        assert s.done == len(s.order) + (1 if s.direct else 2)
-
-    scale = 1.0 / (nodes * patches * reps)
+    assert all(s.complete for s in streams)
     for c in halo_sent + returned[0]:
         c.wait()
-    into = {"ro": (o_ro, 0), "no": (o_nout, 0), "ni": (o_nin, 0), "eo": (o_eout, 0), "c0": (o_ein, 0), "c1": (o_ein, half)}
-    for group, members in groups.items():
-        for s, place in members:
-            s.arrive()
-            take(s, into[group][0], place, scale, into[group][1])
     for s in streams:
         s.finish()
 
 
 STREAMS = (
     ("ro", 1, 1, ("wlh",)),
-    ("no", 1, 2, ("hlw+", "wlh")),
-    ("ni", 1, 2, ("hwl", "lwh+")),
-    ("eo", 1, 2, ("wlh+", "lhW")),
-    ("c0", 3, 1, ("wlh+", "lhW+", "wlh+")),
-    ("c1", 3, 1, ("lwh+", "wlh", "wlh+")),
+    ("no", 1, 2, ("lwh+", "wlh")),
+    ("ni", 1, 2, ("hlw+", "lwh")),
+    ("eo", 1, 2, ("wlh+", "wlh+")),
+    ("c0", 2, 1, ("lwh+", "wlh")),
+    ("c1", 3, 1, ("hlW+", "lwh+", "wlh+")),
 )
 
 
 PLAN = (
     (),
-    ("no_0",),
-    ("no_1",),
-    ("ni_0", "ni_1", "ro_0"),
     (),
-    ("no_1",),
-    ("ro_0",),
+    ("no_0", "no_1"),
+    ("ni_0",),
+    ("ni_1", "ro_0"),
     (),
-    ("eo_0", "no_0"),
-    ("eo_1", "ni_1"),
+    ("no_0", "no_1"),
     (),
-    ("no_1", "ro_0", "back"),
-    ("c0_0", "no_0", "c0_1", "c0_2"),
     ("eo_0",),
-    ("eo_1", "ni_1"),
-    ("c1_0", "c1_1", "c1_2", "ni_0"),
-    ("c0_0", "no_0", "no_1", "ro_0", "c0_1", "c0_2", "eo_0", "c1_1", "node", "c1_0", "c0_0", "eo_1", "c1_2",
-     "c0_2", "ni_0", "ni_1", "c1_1", "no_1", "ro_0", "c1_0", "eo_1", "c0_1", "c1_2", "ni_0", "eo_0", "c0_0",
-     "c0_2", "c1_1", "ni_0", "c1_0", "c1_2", "c1_1"),
+    ("eo_1", "ro_0"),
+    ("back",),
+    (),
+    ("no_0", "c0_0", "ni_1"),
+    ("c0_1", "no_1"),
+    ("ro_0", "eo_0"),
+    (),
+    ("c1_0", "ni_0", "eo_1", "c1_1", "c1_2", "ni_1", "node", "c0_0", "no_0", "eo_0", "no_1", "c0_1", "ro_0",
+     "ni_0", "eo_1", "c1_2", "c1_1", "c0_0", "no_0", "c1_0", "no_1", "ro_0", "c0_1", "ni_0", "no_1", "ro_0",
+     "c1_2", "ni_1", "eo_0", "c1_1", "c1_0", "eo_1", "ni_0", "c0_0", "ni_1", "eo_0", "c0_1", "ni_1", "c1_0",
+     "c1_2", "eo_1", "c1_1", "c0_0", "c0_1", "c1_2", "c0_1", "c1_1"),
 )
 
 
@@ -552,6 +574,8 @@
         pltpu.VMEM((nodes, width), BF16),
         pltpu.VMEM((nodes, width), F32),
         pltpu.VMEM((nodes, variables), F32),
+        *[pltpu.VMEM((nodes, width), BF16)] * 4, pltpu.VMEM((nodes, variables), BF16),
+        *[pltpu.VMEM((nodes, width), F32)] * 2,
         dma(4), dma(4),
     ]
     sizes = {"side": 2, "wide": reps // 2, "low": 2, "high": patches // 2}

time: 47.2 us -> 46.1 us (0.977)
  Pallas kernels: 45.6 us -> 44.5 us
    pallas_call x1, Pallas kernels: 44 us -> 43 us  [call(): pl.pallas_call(functools.partial(kernel, (patches, reps, slot, far, ext,...]
where the time goes in v2:
time: 46.1 us; the launch traced here: 45.9 us
  Pallas kernels  44.5 us (97%)
  between operations  1.45 us (3%)
    pallas_call x1, Pallas kernels, call(): pl.pallas_call(functools.partial(kernel, (patches, reps, slot, far, ext,...  43 us
    pallas_call x1, Pallas kernels, settle(): pl.pallas_call(functools.partial(settle_kernel, n), out_shape=tuple((jax....  1.54 us

profile of v2, /device:TPU:0, one launch (start us, length us, event | category | flops | bytes accessed | tf_op | source)
XLA Modules:
  0.0 45.9 jit_solution(7308809847809418469)
XLA Ops:
  1.3 43.0 %shard_map.198 = (bf16[384,512]{1,0:T(8,128)(2,1)S(1)}, bf16[1280,512]{1,0:T(8,128)(2,1)S(1)}, f32[192,512]{1,0:T(8,128)S(1)}, f32[64,512]{1,0:T(8,128)S(1)}, f3...) custom-call(bf16[384,512]{1,0:T(8,128)(2,1)} %bitcast.6, bf16[1280,512]{1,0:T(8,128)(2,1)} %bitcast.5, ...), custom_call_target="tpu_custom_call" | custom-call | tf_op jit(solution)/shard_map/pallas_call | solution.py:586
  44.2 1.5 %shard_map.199 = (bf16[384,512]{1,0:T(8,128)(2,1)}, bf16[1280,512]{1,0:T(8,128)(2,1)}, f32[192,512]{1,0:T(8,128)}, f32[64,512]{1,0:T(8,128)}, f32[128,512]{1,0:T...) custom-call(bf16[384,512]{1,0:T(8,128)(2,1)S(1)} %get-tuple-element.21.refs_0_, ...), custom_call_target="tpu_custom_call" | custom-call | tf_op jit(solution)/shard_map/pallas_call | solution.py:524

commit v3 on v2

--- a/solution.py
+++ b/solution.py
@@ -479,10 +479,10 @@
 STREAMS = (
     ("ro", 1, 1, ("wlh",)),
     ("no", 1, 2, ("lwh+", "wlh")),
-    ("ni", 1, 2, ("hlw+", "lwh")),
-    ("eo", 1, 2, ("wlh+", "wlh+")),
+    ("ni", 1, 2, ("hlW", "lwh")),
+    ("eo", 1, 2, ("wlh+", "wlh")),
     ("c0", 2, 1, ("lwh+", "wlh")),
-    ("c1", 3, 1, ("hlW+", "lwh+", "wlh+")),
+    ("c1", 3, 1, ("hlw", "wlh+", "lwh+")),
 )
 
 
@@ -504,9 +504,9 @@
     ("ro_0", "eo_0"),
     (),
     ("c1_0", "ni_0", "eo_1", "c1_1", "c1_2", "ni_1", "node", "c0_0", "no_0", "eo_0", "no_1", "c0_1", "ro_0",
-     "ni_0", "eo_1", "c1_2", "c1_1", "c0_0", "no_0", "c1_0", "no_1", "ro_0", "c0_1", "ni_0", "no_1", "ro_0",
-     "c1_2", "ni_1", "eo_0", "c1_1", "c1_0", "eo_1", "ni_0", "c0_0", "ni_1", "eo_0", "c0_1", "ni_1", "c1_0",
-     "c1_2", "eo_1", "c1_1", "c0_0", "c0_1", "c1_2", "c0_1", "c1_1"),
+     "ni_0", "eo_1", "c1_1", "c1_2", "c0_0", "no_0", "c1_0", "no_1", "ro_0", "c0_1", "ni_0", "no_1", "ro_0",
+     "c1_1", "ni_1", "ni_0", "eo_0", "c1_2", "c1_0", "eo_1", "c0_0", "ni_1", "eo_0", "c0_1", "c1_0", "ni_1",
+     "eo_1", "c1_1", "c1_2", "eo_1", "c0_0", "c0_1", "c1_0", "c1_1", "c0_1", "c1_0", "c1_2"),
 )
 
 

time: 46.1 us -> 46.1 us (level)
  no operation moved by 1% of the time
where the time goes in v3:
time: 46.1 us; the launch traced here: 46 us
  Pallas kernels  44.5 us (97%)
  between operations  1.45 us (3%)
    pallas_call x1, Pallas kernels, call(): pl.pallas_call(functools.partial(kernel, (patches, reps, slot, far, ext,...  43 us
    pallas_call x1, Pallas kernels, settle(): pl.pallas_call(functools.partial(settle_kernel, n), out_shape=tuple((jax....  1.54 us

profile of v3, /device:TPU:0, one launch (start us, length us, event | category | flops | bytes accessed | tf_op | source)
XLA Modules:
  0.0 46.0 jit_solution(4080825753892073575)
XLA Ops:
  1.3 43.0 %shard_map.198 = (bf16[384,512]{1,0:T(8,128)(2,1)S(1)}, bf16[1280,512]{1,0:T(8,128)(2,1)S(1)}, f32[192,512]{1,0:T(8,128)S(1)}, f32[64,512]{1,0:T(8,128)S(1)}, f3...) custom-call(bf16[384,512]{1,0:T(8,128)(2,1)} %bitcast.6, bf16[1280,512]{1,0:T(8,128)(2,1)} %bitcast.5, ...), custom_call_target="tpu_custom_call" | custom-call | tf_op jit(solution)/shard_map/pallas_call | solution.py:586
  44.3 1.5 %shard_map.199 = (bf16[384,512]{1,0:T(8,128)(2,1)}, bf16[1280,512]{1,0:T(8,128)(2,1)}, f32[192,512]{1,0:T(8,128)}, f32[64,512]{1,0:T(8,128)}, f32[128,512]{1,0:T...) custom-call(bf16[384,512]{1,0:T(8,128)(2,1)S(1)} %get-tuple-element.21.refs_0_, ...), custom_call_target="tpu_custom_call" | custom-call | tf_op jit(solution)/shard_map/pallas_call | solution.py:524
